TPU v7x, 8 devices: a whole 2x2x1 slice. The times are simulated.
8 devices in a mesh: dp: 1 (over z), tp2: 2 (over y), tp: 4 (over x, core).
Axes of the slice: x: 2, y: 2, z: 1, core: 2. Of those that a mesh axis runs over, the one named last changes fastest.
Arguments:
- hidden: bfloat16 [1024, 4096], P('dp')
- w_gate: bfloat16 [4096, 11008], P(None, ('tp2', 'tp'))
- w_up: bfloat16 [4096, 11008], P(None, ('tp2', 'tp'))
- w_down: bfloat16 [11008, 4096], P(('tp2', 'tp'))
- norm_gain: float32 [4096], replicated
- w_vocab: bfloat16 [4096, 32000], P(None, ('tp2', 'tp'))
- temperature: float32 [1024], P('dp')
- target_ids: int32 [1024], P('dp')
Outputs:
- output 1: float32 [1024], P('dp')
- output 2: float32 [1024], P('dp')
- output 3: float32 [1024], P('dp')
- output 4: bfloat16 [1024, 32000], P('dp', ('tp2', 'tp'))
All inputs are finite; a program needn't handle non-finite values.
Results may differ from a plain program's by a relative error of at most 0.00376407.
Values are sent between devices in bfloat16 or wider.
A program may use at most 1 GiB of HBM per device.

v0:
```python
import functools

import jax
import jax.numpy as jnp
from jax import lax
from jax.experimental import pallas as pl
from jax.experimental.pallas import tpu as pltpu
from jax.sharding import PartitionSpec as P

NORM_EPS = 1e-6
ROWS = 256
CHUNKS = 4
D = 4096
PIECE = 400
FF = 1376
V = 4000
GB = ((0, 256), (256, 256), (512, 512), (1024, 352))
VL = ((2752, 1248), (0, 1024), (1376, 1024), (1024, 352), (2400, 352))
VB = (((2752, 624), (3376, 624)), ((0, 512), (512, 512)), ((1376, 512), (1888, 512)), ((1024, 352), (2400, 352)))
VN = (1248, 1024, 1024, 704)
VR = (((2752, 0, 1248),), ((0, 0, 1024),), ((1376, 0, 1024),), ((1024, 0, 352), (2400, 352, 352)))
f32, bf16 = jnp.float32, jnp.bfloat16
MESH = pl.DeviceIdType.MESH

B1B_LATE = False
TABLE = {
    (1, 1, 0): [('E1a', 0)],
    (1, 1, 2): [('E1b', 0)],
    (1, 1, 3): [('E2a', 0)],
    (1, 2, 0): [('E3', 0)],
    (1, 2, 2): [('E1b', 1)],
    (1, 3, 1): [('E3', 1)],
    (2, 1, 1): [('E2b', 0), ('E1a', 1)],
    (2, 2, 0): [('E2a', 1), ('E4', 0)],
    (2, 2, 1): [('E2b', 1), ('E1a', 2)],
    (2, 3, 0): [('E1b', 2), ('E5', 0)],
    (2, 3, 1): [('E2a', 2), ('E6', 0)],
    (3, 0, 0): [('E7', 0), ('E4', 1)],
    (3, 0, 1): [('E2b', 2), ('E1a', 3)],
    (3, 0, 2): [('E1b', 3), ('E5', 1)],
    (3, 0, 3): [('E6', 1), ('E3', 2)],
    (3, 1, 0): [('E7', 1)],
    (3, 1, 1): [('E2a', 3), ('E2b', 3)],
    (3, 1, 2): [('E4', 2)],
    (3, 1, 3): [('E5', 2), ('E3', 3)],
    (3, 2, 0): [('E6', 2), ('E7', 2)],
    (3, 2, 1): [('E4', 3)],
    (3, 2, 2): [('E5', 3)],
    (3, 2, 3): [('E6', 3)],
    (3, 3, 0): [('E7', 3)],
}

KD, KB1A, KB1B, KB2, KA1, KA2A, KA2B, KA3A, KA3B, KA3C, KA3D = 0, 2, 4, 6, 8, 9, 10, 11, 12, 13, 14
NK = 15


def kernel(hid, wg, wu, wd, gain, wv, temp, tgt, out, last_l, stats,
           X, PB, DR, B1, B2, W, rsc, ST, SR,
           ssem, rsem, st_s, st_r, xsem, gsem, vsem, credit):
    dp = lax.axis_index('dp')
    y = lax.axis_index('tp2')
    tpi = lax.axis_index('tp')
    x = tpi // 2
    c = tpi % 2
    me = y * 4 + tpi
    f = x + c * (y - x)
    s = y + c * (x - y)
    partner = (dp, y, x * 2 + (1 - c))
    nbr1 = (dp, y + c * (1 - 2 * y), (x + (1 - c) * (1 - 2 * x)) * 2 + c)
    nbr2 = (dp, y + (1 - c) * (1 - 2 * y), (x + c * (1 - 2 * x)) * 2 + c)
    half = c * 128

    def al(v, n):
        return pl.multiple_of(v, n)

    def q(fp, sp):
        return al((2 * fp + sp) * 32, 32)

    def xload(i):
        return pltpu.make_async_copy(hid.at[pl.ds(i * ROWS, ROWS), :], X.at[pl.ds(i * ROWS, ROWS), :], xsem.at[i])

    def gload(b, k):
        src, base = ((wg, 0), (wu, FF))[k]
        r0, n = GB[b]
        return pltpu.make_async_copy(src.at[pl.ds(r0, n), :], W.at[pl.ds(base + r0, n), :], gsem.at[b, k])

    def vload(t):
        r0, n = VL[t]
        return pltpu.make_async_copy(wv.at[pl.ds(r0, n), :], W.at[pl.ds(r0, n), :], vsem.at[t])

    def remote(src, dst, i, k, dev):
        return pltpu.make_async_remote_copy(src_ref=src, dst_ref=dst, send_sem=ssem.at[i, k], recv_sem=rsem.at[i, k],
                                            device_id=dev, device_id_type=MESH)

    def xrows(i, fp, sp, hb):
        return X.at[pl.ds(al(i * ROWS + hb + q(fp, sp), 32), 32), :]

    def prow(i, fp, sp, cs):
        return PB.at[lax.rem(i, 2), pl.ds(al(half + q(fp, sp), 32), 32), cs]

    def copy(i, k):
        sl = lax.rem(i, 2)
        if k < KA1:
            kind = k - k % 2
            cs = pl.ds(2048 * (k % 2), 2048)
            if kind == KD:
                return remote(PB.at[sl, pl.ds(al(128 - half, 128), 128), cs], DR.at[sl, :, cs], i, k, partner)
            if kind == KB1A:
                return remote(prow(i, 1 - f, 1 - s, cs), B1.at[sl, 0, :, cs], i, k, nbr1)
            if kind == KB1B:
                return remote(prow(i, 1 - f, s, cs), B1.at[sl, 1, :, cs], i, k, nbr1)
            return remote(prow(i, f, 1 - s, cs), B2.at[sl, :, cs], i, k, nbr2)
        fp, sp = {KA1: (f, s), KA2A: (f, s), KA3A: (f, s), KA2B: (f, 1 - s), KA3B: (f, 1 - s),
                  KA3C: (1 - f, s), KA3D: (1 - f, 1 - s)}[k]
        dev = {KA1: nbr2, KA2A: nbr1, KA2B: nbr1}.get(k, partner)
        r = xrows(i, fp, sp, half)
        return remote(r, r, i, k, dev)

    def e1(i, h):
        copy(i, KD + h).wait_recv()
        sl = lax.rem(i, 2)
        for sp, k in ((1 - s, KB1A), (s, KB1B)):
            r0 = q(1 - f, sp)

            def add(t, carry):
                pr = pl.ds(al(half + r0 + t * 16, 16), 16)
                dr = pl.ds(al(r0 + t * 16, 16), 16)
                for cb in range(2):
                    cs = slice(2048 * h + cb * 1024, 2048 * h + cb * 1024 + 1024)
                    PB[sl, pr, cs] = (PB[sl, pr, cs].astype(f32) + DR[sl, dr, cs].astype(f32)).astype(bf16)
                return carry

            lax.fori_loop(0, 2, add, 0)
            if k == KB1A and i >= 2 and h == 0:
                pl.semaphore_wait(credit.at[1], 1)
            if k == KB1A or not B1B_LATE:
                copy(i, k + h).start()

    def e2(i, h):
        copy(i, KB1A + h).wait_recv()
        sl = lax.rem(i, 2)
        r0 = q(f, 1 - s)

        def add(t, carry):
            pr = pl.ds(al(half + r0 + t * 16, 16), 16)
            dr = pl.ds(al(r0 + t * 16, 16), 16)
            br = pl.ds(al(t * 16, 16), 16)
            for cb in range(2):
                cs = slice(2048 * h + cb * 1024, 2048 * h + cb * 1024 + 1024)
                PB[sl, pr, cs] = (PB[sl, pr, cs].astype(f32) + DR[sl, dr, cs].astype(f32)
                                  + B1[sl, 0, br, cs].astype(f32)).astype(bf16)
            return carry

        lax.fori_loop(0, 2, add, 0)
        if i >= 2 and h == 0:
            pl.semaphore_wait(credit.at[2], 1)
        copy(i, KB2 + h).start()
        if B1B_LATE:
            copy(i, KB1B + h).start()

    def e3(i):
        for h in range(2):
            copy(i, KB1B + h).wait_recv()
            copy(i, KB2 + h).wait_recv()
        sl = lax.rem(i, 2)
        r0 = q(f, s)

        def fin(t, carry):
            pr = pl.ds(al(half + r0 + t * 16, 16), 16)
            dr = pl.ds(al(r0 + t * 16, 16), 16)
            br = pl.ds(al(t * 16, 16), 16)
            xr = pl.ds(al(i * ROWS + half + r0 + t * 16, 16), 16)
            acc = jnp.zeros((16, 128), f32)
            for cb in range(16):
                cs = slice(cb * 256, cb * 256 + 256)
                part = (PB[sl, pr, cs].astype(f32) + DR[sl, dr, cs].astype(f32)
                        + B1[sl, 1, br, cs].astype(f32) + B2[sl, br, cs].astype(f32)).astype(bf16)
                r = X[xr, cs].astype(f32) + part.astype(f32)
                rsc[:, cs] = r
                sq = r * r
                acc = acc + sq[:, :128] + sq[:, 128:]
            ms = jnp.sum(acc, axis=1, keepdims=True) * (1.0 / D)
            inv = lax.rsqrt(ms + NORM_EPS)
            for cb in range(16):
                cs = slice(cb * 256, cb * 256 + 256)
                X[xr, cs] = (gain[:, cs] * rsc[:, cs] * inv).astype(bf16)
            return carry

        lax.fori_loop(0, 2, fin, 0)
        copy(i, KA1).start()
        copy(i, KA2A).start()
        copy(i, KA3A).start()
        if i < 2:
            for n, dev in ((0, partner), (1, nbr1), (2, nbr2)):
                pl.semaphore_signal(credit.at[n], inc=1, device_id=dev, device_id_type=MESH)

    def e4(i):
        copy(i, KA1).wait_recv()
        copy(i, KA2B).start()
        copy(i, KA3B).start()

    def e5(i):
        copy(i, KA2A).wait_recv()
        copy(i, KA3C).start()

    def e6(i):
        copy(i, KA2B).wait_recv()
        copy(i, KA3D).start()

    def e7(i):
        for k in (KA3A, KA3B, KA3C, KA3D):
            copy(i, k).wait_recv()

    events = {'E3': e3, 'E4': e4, 'E5': e5, 'E6': e6, 'E7': e7}
    for h_, n_ in ((0, 'a'), (1, 'b')):
        events['E1' + n_] = functools.partial(e1, h=h_)
        events['E2' + n_] = functools.partial(e2, h=h_)

    def progress(phase, i, b):
        for ck in range(CHUNKS):
            todo = TABLE.get((phase, ck, b), [])
            if todo:
                @pl.when(i == ck)
                def _():
                    for name, cc in todo:
                        events[name](cc)

    xload(0).start()
    for b in range(2):
        for k in range(2):
            gload(b, k).start()

    def dott(w, xv):
        return lax.dot_general(w, xv, (((1,), (1,)), ((), ())), preferred_element_type=f32)

    def phase1(wdv, act, dsem):
        def dload(k):
            cs = pl.ds(2048 * k, 2048)
            return pltpu.make_async_copy(wd.at[:, cs], wdv.at[:, cs], dsem.at[k])


        bar = pltpu.get_barrier_semaphore()
        for d in range(1, 8):
            o = (me + d) % 8
            pl.semaphore_signal(bar, inc=1, device_id=(dp, o // 4, o % 4), device_id_type=MESH)
        pl.semaphore_wait(bar, 7)
        for k in range(2):
            gload(2, k).start()

        def chunk(i, carry):
            rows = pl.ds(al(i * ROWS, ROWS), ROWS)
            sl = lax.rem(i, 2)
            xload(i).wait()

            def first(fn):
                pl.when(i == 0)(fn)

            def last(fn):
                pl.when(i == CHUNKS - 1)(fn)

            for b, (r0, n) in enumerate(GB):
                @first
                def _():
                    for k in range(2):
                        gload(b, k).wait()
                    for cp in ((gload(3, 0), gload(3, 1)), (dload(0), dload(1)), (xload(1), xload(2), xload(3)), ())[b]:
                        cp.start()

                progress(1, i, b)
                g = dott(W[r0:r0 + n, :], X[rows, :])
                u = dott(W[FF + r0:FF + r0 + n, :], X[rows, :])
                h = g * jax.nn.sigmoid(g) * u
                act[:, r0:r0 + n] = jnp.transpose(h.astype(bf16))

                @last
                def _():
                    for t in ((), (), (1, 2), (3, 4))[b]:
                        vload(t).start()

            @first
            def _():
                vload(0).start()

            for b in range(2):
                first(lambda: dload(b).wait())
                progress(2, i, b)
                if b == 0:
                    @pl.when(i >= 2)
                    def _():
                        for k in range(KA1):
                            copy(i - 2, k).wait_send()
                        pl.semaphore_wait(credit.at[0], 1)

                for n in range(8):
                    cs = slice(2048 * b + 256 * n, 2048 * b + 256 * n + 256)
                    PB[sl, :, cs] = jnp.dot(act[...], wdv[:, cs], preferred_element_type=f32).astype(bf16)

                copy(i, KD + b).start()

            return carry

        lax.fori_loop(0, CHUNKS, chunk, 0)

    pl.run_scoped(phase1, pltpu.VMEM((FF, D), bf16), pltpu.VMEM((ROWS, FF), bf16), pltpu.SemaphoreType.DMA((2,)))

    def phase2(L0, L1, L2, L3, OS, state, IT, TG, LN, osem, lsem):
        L = (L0, L1, L2, L3)
        sub = lax.broadcasted_iota(jnp.int32, (8, ROWS), 0)

        def stats_block(cur, b):
            groups = [(lo + k, v + k) for v, lo, n in VR[b] for k in range(0, n, 8)]
            ms = [L[b][cur, r:r + 8, :] for r, _ in groups[:4]]
            for k, (r, _) in enumerate(groups[4:]):
                ms[k % 4] = jnp.maximum(ms[k % 4], L[b][cur, r:r + 8, :])
            m_new = jnp.maximum(jnp.maximum(ms[0], ms[1]), jnp.maximum(ms[2], ms[3]))
            zero = jnp.zeros((8, ROWS), f32)
            ss, ws, ts = [zero] * 2, [zero] * 2, [zero] * 2
            if b > 0:
                m_old = state[0]
                m_new = jnp.maximum(m_new, m_old)
                scale = jnp.exp(m_old - m_new)
                ss[0], ws[0], ts[0] = state[1] * scale, state[2] * scale, state[3]
            tg = TG[...] - sub
            for k, (r, v) in enumerate(groups):
                l = L[b][cur, r:r + 8, :]
                e = jnp.exp(l - m_new)
                ss[k % 2] = ss[k % 2] + e
                ws[k % 2] = ws[k % 2] + e * l
                ts[k % 2] = jnp.where(tg == v, l, ts[k % 2])
            state[0] = m_new
            state[1] = ss[0] + ss[1]
            state[2] = ws[0] + ws[1]
            state[3] = ts[0] + ts[1]

        def final_block(old, b):
            for v, lo, n in VR[b]:
                for k in range(0, n, 16):
                    OS[v + k:v + k + 16, :] = (L[b][old, lo + k:lo + k + 16, :] - LN[0:1, :]).astype(bf16)

        def ocopies(i, blocks):
            return [pltpu.make_async_copy(OS.at[pl.ds(v, n), :], out.at[pl.ds(v, n), pl.ds(al(i * ROWS, ROWS), ROWS)],
                                          osem.at[b, k]) for b in blocks for k, (v, lo, n) in enumerate(VR[b])]

        def lcopies(b):
            return [pltpu.make_async_copy(L[b].at[(CHUNKS - 1) % 2, pl.ds(lo, n), :], last_l.at[pl.ds(v, n), :], lsem.at[b, k])
                    for k, (v, lo, n) in enumerate(VR[b])]

        def stat_copy(i, d):
            o = (me + d) % 8
            return pltpu.make_async_remote_copy(src_ref=ST.at[i], dst_ref=SR.at[i, me], send_sem=st_s.at[i, d],
                                                recv_sem=st_r.at[i, me],
                                                device_id=(dp, o // 4, o % 4), device_id_type=MESH)

        def stat_wait(i, d):
            o = (me + d) % 8
            return pltpu.make_async_remote_copy(src_ref=ST.at[i], dst_ref=SR.at[i, o], send_sem=st_s.at[i, d],
                                                recv_sem=st_r.at[i, o],
                                                device_id=(dp, o // 4, o % 4), device_id_type=MESH)

        def send_stats(i):
            m = state[0]
            mx = jnp.max(m, axis=0, keepdims=True)
            e = jnp.exp(m - mx)
            row = lax.broadcasted_iota(jnp.int32, (8, ROWS), 0)
            pk = jnp.broadcast_to(mx, (8, ROWS))
            for n in (1, 2, 3):
                v = state[n] * e if n < 3 else state[n]
                pk = jnp.where(row == n, jnp.sum(v, axis=0, keepdims=True), pk)
            ST[i] = pk
            SR[i, me] = pk
            for d in range(1, 8):
                stat_copy(i, d).start()

        def recv_stats(i):
            for d in range(1, 8):
                stat_wait(i, d).wait_recv()
            parts = [SR[i, o] for o in range(8)]
            mg = parts[0][0:1, :]
            for p_ in parts[1:]:
                mg = jnp.maximum(mg, p_[0:1, :])
            sg = wgt = tl = jnp.zeros((1, ROWS), f32)
            for p_ in parts:
                e = jnp.exp(p_[0:1, :] - mg)
                sg = sg + p_[1:2, :] * e
                wgt = wgt + p_[2:3, :] * e
                tl = tl + p_[3:4, :]
            lg = mg + jnp.log(sg)
            cs = pl.ds(al(i * ROWS, ROWS), ROWS)
            stats[0:1, cs] = lg
            stats[1:2, cs] = lg - wgt / sg
            stats[2:3, cs] = tl - lg
            LN[...] = jnp.broadcast_to(lg, (8, ROWS))

        def chunk(j, carry):
            rows = pl.ds(al(j * ROWS, ROWS), ROWS)
            cur, old = lax.rem(j, 2), lax.rem(j + 1, 2)
            cs = pl.ds(al(j * ROWS, ROWS), ROWS)
            IT[...] = jnp.broadcast_to(1.0 / temp[:, cs], (8, ROWS))
            tid = tgt[:, cs] - me * V
            TG[...] = jnp.broadcast_to(tid, (8, ROWS))

            def vblock(b):
                lo = 0
                for r0, n in VB[b]:
                    L[b][cur, lo:lo + n, :] = dott(W[r0:r0 + n, :], X[rows, :]) * IT[0:1, :]
                    lo += n

            for b in range(4):
                @pl.when(j == 0)
                def _():
                    for t in ((0,), (1,), (2,), (3, 4))[b]:
                        vload(t).wait()

                progress(3, j, b)
                if b == 3:
                    @pl.when(j >= 2)
                    def _():
                        for cp in ocopies(j - 2, range(4)):
                            cp.wait()

                    @pl.when(j >= 1)
                    def _():
                        recv_stats(j - 1)

                vblock(b)
                if b >= 1:
                    stats_block(cur, b - 1)
                if b == 3:
                    done = range(4)
                    for d in done:
                        final_block(old, d)

                    @pl.when(j >= 1)
                    def _():
                        for cp in ocopies(j - 1, done):
                            cp.start()

                @pl.when(j == CHUNKS - 1)
                def _():
                    for cp in lcopies(b):
                        cp.start()

            stats_block(cur, 3)
            send_stats(j)
            return carry

        lax.fori_loop(0, CHUNKS, chunk, 0)
        for i in range(CHUNKS):
            for k in range(NK):
                if k >= KA1 or i >= 2:
                    copy(i, k).wait_send()
        for cp in ocopies(CHUNKS - 2, range(4)):
            cp.wait()
        for b in range(4):
            for cp in lcopies(b):
                cp.wait()
        recv_stats(CHUNKS - 1)
        for i in range(CHUNKS):
            for d in range(1, 8):
                stat_copy(i, d).wait_send()

    pl.run_scoped(phase2, *[pltpu.VMEM((2, n, ROWS), f32) for n in VN], pltpu.VMEM((V, ROWS), bf16),
                  pltpu.VMEM((4, 8, ROWS), f32), pltpu.VMEM((8, ROWS), f32), pltpu.VMEM((8, ROWS), jnp.int32),
                  pltpu.VMEM((8, ROWS), f32), pltpu.SemaphoreType.DMA((4, 2)), pltpu.SemaphoreType.DMA((4, 2)))


def finish(lp, l, st_ref, out, s0, s1, s2, lpv, lv, ov, isem, jsem, osem, psem):
    n = lpv.shape[1]
    pieces = range(V // PIECE)

    def rows(k):
        return pl.ds(k * PIECE, PIECE)

    early = [pltpu.make_async_copy(lp.at[rows(k), pl.ds(0, n)], lpv.at[rows(k), :], isem.at[k]) for k in pieces]
    late = [pltpu.make_async_copy(l.at[rows(k), :], lv.at[rows(k), :], jsem.at[k]) for k in pieces]
    put = [pltpu.make_async_copy(lpv.at[rows(k), :], out.at[rows(k), pl.ds(0, n)], osem.at[k]) for k in pieces]
    end = [pltpu.make_async_copy(ov.at[rows(k), :], out.at[rows(k), pl.ds(n, ROWS)], psem.at[k]) for k in pieces]
    for k in pieces:
        early[k].start()
        late[k].start()
    s0[...] = st_ref[0:1, :]
    s1[...] = st_ref[1:2, :]
    s2[...] = st_ref[2:3, :]
    for k in pieces:
        early[k].wait()
        put[k].start()
        late[k].wait()
        r = k * PIECE
        ov[r:r + PIECE, :] = (lv[r:r + PIECE, :] - st_ref[0:1, n:]).astype(bf16)
        end[k].start()
    for k in pieces:
        put[k].wait()
        end[k].wait()


def solution(mesh):
    model_axes = ('tp2', 'tp')

    def local_step(hidden, w_gate, w_up, w_down, norm_gain, w_vocab, temperature, target_ids):
        n = hidden.shape[0]
        anyspec = pl.BlockSpec(memory_space=pl.ANY)
        vspec = pl.BlockSpec(memory_space=pltpu.VMEM)
        early, last_l, stats = pl.pallas_call(
            kernel,
            out_shape=(jax.ShapeDtypeStruct((V, n), bf16), jax.ShapeDtypeStruct((V, ROWS), f32),
                       jax.ShapeDtypeStruct((8, n), f32)),
            in_specs=[anyspec, anyspec, anyspec, anyspec, vspec, anyspec, vspec, vspec],
            out_specs=(anyspec, anyspec, vspec),
            scratch_shapes=[
                pltpu.VMEM((n, D), bf16),
                pltpu.VMEM((2, ROWS, D), bf16),
                pltpu.VMEM((2, ROWS // 2, D), bf16),
                pltpu.VMEM((2, 2, ROWS // 8, D), bf16),
                pltpu.VMEM((2, ROWS // 8, D), bf16),
                pltpu.VMEM((V, D), bf16),
                pltpu.VMEM((16, D), f32),
                pltpu.VMEM((CHUNKS, 8, ROWS), f32),
                pltpu.VMEM((CHUNKS, 8, 8, ROWS), f32),
                pltpu.SemaphoreType.DMA((CHUNKS, NK)),
                pltpu.SemaphoreType.DMA((CHUNKS, NK)),
                pltpu.SemaphoreType.DMA((CHUNKS, 8)),
                pltpu.SemaphoreType.DMA((CHUNKS, 8)),
                pltpu.SemaphoreType.DMA((CHUNKS,)),
                pltpu.SemaphoreType.DMA((4, 2)),
                pltpu.SemaphoreType.DMA((5,)),
                pltpu.SemaphoreType.REGULAR((3,)),
            ],
            compiler_params=pltpu.CompilerParams(collective_id=0, has_side_effects=True, vmem_limit_bytes=67043328),
        )(hidden, w_gate.T, w_up.T, w_down, norm_gain.reshape(1, D), w_vocab.T,
          temperature.reshape(1, n), target_ids.reshape(1, n))
        dma = pltpu.SemaphoreType.DMA((V // PIECE,))
        logprobs, s0, s1, s2 = pl.pallas_call(
            finish,
            out_shape=(jax.ShapeDtypeStruct((V, n), bf16),) + (jax.ShapeDtypeStruct((1, n), f32),) * 3,
            in_specs=[anyspec, anyspec, vspec],
            out_specs=(anyspec, vspec, vspec, vspec),
            scratch_shapes=[pltpu.VMEM((V, n - ROWS), bf16), pltpu.VMEM((V, ROWS), f32), pltpu.VMEM((V, ROWS), bf16),
                            dma, dma, dma, dma],
            compiler_params=pltpu.CompilerParams(vmem_limit_bytes=67043328),
        )(early, last_l, stats)
        return s0.reshape(n), s1.reshape(n), s2.reshape(n), logprobs.T

    return jax.shard_map(
        local_step, mesh=mesh,
        in_specs=(P('dp', None), P(None, model_axes), P(None, model_axes), P(model_axes, None),
                  P(None), P(None, model_axes), P('dp'), P('dp')),
        out_specs=(P('dp'), P('dp'), P('dp'), P('dp', model_axes)),
        check_vma=False)
```

profile of v0, /device:TPU:0, one launch (start us, length us, event | category | flops | bytes accessed | tf_op | source)
XLA Modules:
  0.0 122.2 jit_solution(13456972997484875438)
XLA Ops:
  0.6 112.7 %shard_map.111 = (bf16[4000,1024]{1,0:T(8,128)(2,1)}, f32[4000,256]{1,0:T(8,128)}, f32[8,1024]{1,0:T(8,128)}) custom-call(bf16[1024,4096]{1,0:T(8,128)(2,1)} %hid.1, bf16[1376,4096]{1,0:T(8,128)(2,1)} %bitcast.11, bf16[1376,4096]{1,0:T(8,128)(2,1)} %bitcast.12, bf16[1376,4096]{1,0:T(8,128)(2,1)} %wd.1, f32[1,4096]{1,0:T(1,128)} %bitcast.13, ...), custom_call_target="tpu_custom_call" | custom-call | tf_op jit(solution)/shard_map/pallas_call | solution.py:503
  113.4 8.7 %shard_map.112 = (bf16[4000,1024]{1,0:T(8,128)(2,1)}, f32[1,1024]{1,0:T(1,128)}, f32[1,1024]{1,0:T(1,128)}, f32[1,1024]{1,0:T(1,128)}) custom-call(bf16[4000,1024]{1,0:T(8,128)(2,1)} %get-tuple-element.11.lp, f32[4000,256]{1,0:T(8,128)} %get-tuple-element.12.l, f32[8,1024]{1,0:T(8,128)} %get-tuple-element.13.st_ref), custom_call_target="tpu_custom_call" | custom-call | tf_op jit(solution)/shard_map/pallas_call | solution.py:532
where the time goes:
time: 122 us
  Pallas kernels  121 us (99%)
    pallas_call x1, Pallas kernels, local_step(): pl.pallas_call(kernel, out_shape=(jax.ShapeDtypeStruct((V, n), bf16), jax...  113 us
    pallas_call x1, Pallas kernels, local_step(): pl.pallas_call(finish, out_shape=(jax.ShapeDtypeStruct((V, n), bf16),) +...  8.69 us

commit v1 on v0

--- a/solution.py
+++ b/solution.py
@@ -27,23 +27,23 @@
     (1, 1, 0): [('E1a', 0)],
     (1, 1, 2): [('E1b', 0)],
     (1, 1, 3): [('E2a', 0)],
+    (2, 1, 1): [('E2b', 0), ('E1a', 1)],
     (1, 2, 0): [('E3', 0)],
     (1, 2, 2): [('E1b', 1)],
-    (1, 3, 1): [('E3', 1)],
-    (2, 1, 1): [('E2b', 0), ('E1a', 1)],
     (2, 2, 0): [('E2a', 1), ('E4', 0)],
     (2, 2, 1): [('E2b', 1), ('E1a', 2)],
+    (1, 3, 1): [('E3', 1)],
     (2, 3, 0): [('E1b', 2), ('E5', 0)],
     (2, 3, 1): [('E2a', 2), ('E6', 0)],
     (3, 0, 0): [('E7', 0), ('E4', 1)],
-    (3, 0, 1): [('E2b', 2), ('E1a', 3)],
-    (3, 0, 2): [('E1b', 3), ('E5', 1)],
+    (3, 0, 1): [('E1a', 3)],
+    (3, 0, 2): [('E1b', 3), ('E2b', 2), ('E5', 1)],
     (3, 0, 3): [('E6', 1), ('E3', 2)],
     (3, 1, 0): [('E7', 1)],
     (3, 1, 1): [('E2a', 3), ('E2b', 3)],
     (3, 1, 2): [('E4', 2)],
-    (3, 1, 3): [('E5', 2), ('E3', 3)],
-    (3, 2, 0): [('E6', 2), ('E7', 2)],
+    (3, 1, 3): [('E3', 3)],
+    (3, 2, 0): [('E5', 2), ('E6', 2), ('E7', 2)],
     (3, 2, 1): [('E4', 3)],
     (3, 2, 2): [('E5', 3)],
     (3, 2, 3): [('E6', 3)],

time: 122 us -> 122 us (level)
  no operation moved by 1% of the time
where the time goes in v1:
time: 122 us
  Pallas kernels  121 us (99%)
    pallas_call x1, Pallas kernels, local_step(): pl.pallas_call(kernel, out_shape=(jax.ShapeDtypeStruct((V, n), bf16), jax...  113 us
    pallas_call x1, Pallas kernels, local_step(): pl.pallas_call(finish, out_shape=(jax.ShapeDtypeStruct((V, n), bf16),) +...  8.69 us

profile of v1, /device:TPU:0, one launch (start us, length us, event | category | flops | bytes accessed | tf_op | source)
XLA Modules:
  0.0 122.2 jit_solution(7026923492015777091)
XLA Ops:
  0.6 112.7 %shard_map.111 = (bf16[4000,1024]{1,0:T(8,128)(2,1)}, f32[4000,256]{1,0:T(8,128)}, f32[8,1024]{1,0:T(8,128)}) custom-call(bf16[1024,4096]{1,0:T(8,128)(2,1)} %hid.1, bf16[1376,4096]{1,0:T(8,128)(2,1)} %bitcast.11, bf16[1376,4096]{1,0:T(8,128)(2,1)} %bitcast.12, bf16[1376,4096]{1,0:T(8,128)(2,1)} %wd.1, f32[1,4096]{1,0:T(1,128)} %bitcast.13, ...), custom_call_target="tpu_custom_call" | custom-call | tf_op jit(solution)/shard_map/pallas_call | solution.py:503
  113.4 8.7 %shard_map.112 = (bf16[4000,1024]{1,0:T(8,128)(2,1)}, f32[1,1024]{1,0:T(1,128)}, f32[1,1024]{1,0:T(1,128)}, f32[1,1024]{1,0:T(1,128)}) custom-call(bf16[4000,1024]{1,0:T(8,128)(2,1)} %get-tuple-element.11.lp, f32[4000,256]{1,0:T(8,128)} %get-tuple-element.12.l, f32[8,1024]{1,0:T(8,128)} %get-tuple-element.13.st_ref), custom_call_target="tpu_custom_call" | custom-call | tf_op jit(solution)/shard_map/pallas_call | solution.py:532
